TPU v7x, 256 devices: a whole 4x4x8 slice. The times are simulated.
256 devices in a mesh: band: 16 (over z, y_lo), grid: 16 (over x, y_hi, core).
Axes of the slice: x: 4, y: 4 (y_hi: 2, y_lo: 2; y = y_hi * 2 + y_lo), z: 8, core: 2. Of those that a mesh axis runs over, the one named last changes fastest.
Arguments:
- orbitals: bfloat16 [16, 128, 128, 128], P('band', 'grid'), may hold values from -3 to 3
- trial_vectors: bfloat16 [2, 16, 128, 128, 128], P(None, 'band', 'grid'), may hold values from -6 to 6
- alda_kernel: float32 [128, 128, 128], P('grid'), may hold values from -2 to -0.5
- local_potential: float32 [128, 128, 128], P('grid'), may hold values from -2 to 1
- band_energies: float32 [16], P('band'), may hold values from -1.5 to -0.2
Outputs:
- sigma_real: float32 [2, 16, 128, 128, 128], P(None, 'band', 'grid')
- sigma_imag: float32 [2, 16, 128, 128, 128], P(None, 'band', 'grid')
All inputs are finite; a program needn't handle non-finite values.
Results may differ from a plain program's by a relative error of at most 0.0003.
Values sent between devices are 32-bit elements; how exact they have to be, the bound alone decides.
No kernel may reach another device: no remote copies, remote signals or barrier semaphores. Data moves between devices by JAX's collectives and lax.ppermute only.
A program may use at most 64 MiB of HBM per device.

v0:
```python
import functools
import math

import jax
import jax.numpy as jnp
import numpy as np
from jax import lax
from jax.experimental import pallas as pl
from jax.experimental.pallas import tpu as pltpu
from jax.sharding import PartitionSpec as P


box_length = 30.0
NARROW = jnp.bfloat16
WIDE = jnp.float32
ROWS = 8
GRANT = 20 * 2**20
WIDE_GRANT = 60 * 2**20


def halves(table):
    high = table.astype(np.float32).astype(jnp.bfloat16)
    low = (table - high.astype(np.float64)).astype(np.float32).astype(jnp.bfloat16)
    return np.stack([high, low])


@functools.cache
def make_tables(length):
    wrapped = np.outer(np.arange(length), np.arange(length)) % length
    angles = wrapped.astype(np.float64) * (2.0 * math.pi / length)
    cosine, sine = np.cos(angles), np.sin(angles)
    return {
        "down": halves(np.block([[cosine, sine], [-sine, cosine]])),
        "up": halves(np.block([[cosine, -sine], [sine, cosine]])),
        "last": halves(np.block([[cosine, -sine], [sine, cosine]]) * float(length) ** -1.5),
    }


def split(value):
    high = value.astype(NARROW)
    return high, (value - high.astype(WIDE)).astype(NARROW)


def mul(left, right):
    return lax.dot_general(left, right, (((1,), (0,)), ((), ())), preferred_element_type=WIDE)


def product(left, right):
    left_high, left_low = left
    right_high, right_low = right
    return mul(left_high, right_high) + mul(left_low, right_high) + mul(left_high, right_low)


def pair(ref):
    return ref[0], ref[1]


def swap_blocks(value):
    rows, columns = value.shape[0] // 2, value.shape[1] // 2
    left = jnp.concatenate([value[:rows, :columns], value[rows:, :columns]], axis=1)
    right = jnp.concatenate([value[:rows, columns:], value[rows:, columns:]], axis=1)
    return jnp.concatenate([left, right], axis=0)


def parts_down(value):
    half = value.shape[1] // 2
    return jnp.concatenate([value[:, :half], value[:, half:]], axis=0)


def parts_across(value):
    half = value.shape[0] // 2
    return jnp.concatenate([value[:half], value[half:]], axis=1)


def density_kernel(me_ref, orbital_in, trial_in, up_in, down_in, *refs):
    (
        kept_hbm, near_hbm, out_hbm, orbital_ref, trial_ref, up_ref, down_ref, mixed_ref, out_ref,
        table_sems, row_sems, out_sems,
    ) = refs
    me = me_ref[0]
    length = orbital_ref.shape[2]
    parts, share = out_ref.shape[0], out_ref.shape[3]
    half = orbital_ref.shape[1] // 2
    tables = [
        pltpu.make_async_copy(up_in, up_ref, table_sems.at[0]),
        pltpu.make_async_copy(down_in, down_ref, table_sems.at[1]),
    ]
    rows = [pl.ds(i * half, half) for i in range(2)]
    orbitals, trials = [], []
    for i in range(2):
        part = (slice(None), rows[i])
        orbitals.append(
            pltpu.make_async_copy(orbital_in.at[part], orbital_ref.at[part], row_sems.at[i, 0])
        )
        part = (slice(None), slice(None), rows[i])
        trials.append(
            pltpu.make_async_copy(trial_in.at[part], trial_ref.at[part], row_sems.at[i, 1])
        )
    outs = [
        [
            pltpu.make_async_copy(mixed_ref.at[1], near_hbm, out_sems.at[1]),
            pltpu.make_async_copy(mixed_ref.at[0], kept_hbm, out_sems.at[0]),
        ],
        [pltpu.make_async_copy(out_ref, out_hbm, out_sems.at[2])],
    ]
    for copy in (tables[0], orbitals[0], trials[0], tables[1], orbitals[1], trials[1]):
        copy.start()
    for copy in tables:
        copy.wait()
    for i in range(2):
        orbitals[i].wait()
        trials[i].wait()
        values = []
        for x in range(half):
            orbital = 2.0 * orbital_ref[0, i * half + x].astype(WIDE)
            values.append(
                jnp.concatenate(
                    [trial_ref[k, 0, i * half + x].astype(WIDE) * orbital for k in range(2)], axis=1
                )
            )
        turned = product(split(jnp.concatenate(values, axis=0)), pair(up_ref))
        columns = [parts_down(turned[x * length : (x + 1) * length]) for x in range(half)]
        turned = product(pair(down_ref), split(jnp.concatenate(columns, axis=1)))
        for x in range(half):
            for part in range(2):
                block = turned[part * length : (part + 1) * length, x * length : (x + 1) * length]
                if i == 1:
                    out_ref[:, part, x] = block.reshape(parts, share, length)
                    continue
                for n in range(parts):
                    tile = block[n * share : (n + 1) * share]
                    mixed_ref[(n ^ me) & 1, (n ^ me) >> 1, part, x] = tile
        for copy in outs[i]:
            copy.start()
    for copy in outs[0] + outs[1]:
        copy.wait()


def share_kernel(pieces_ref, *refs):
    *near_refs, share_ref, out_ref = refs
    first = near_refs[0][...]
    for ref in near_refs[1:]:
        first = first + ref[...]
    second = pieces_ref[0]
    for i in range(1, pieces_ref.shape[0]):
        second = second + pieces_ref[i]
    rows = first.shape[0] // 2
    for part in range(2):
        held = slice(part * rows, (part + 1) * rows)
        share_ref[2 * part * rows : (2 * part + 1) * rows, :] = first[held]
        share_ref[(2 * part + 1) * rows : 2 * (part + 1) * rows, :] = second[held]
    copies, rows, _ = out_ref.shape
    share = rows // 2
    for b in range(share):
        block = share_ref[pl.ds(b, rows, stride=share), :]
        for i in range(copies // share):
            out_ref[b * (copies // share) + i] = block


def line_kernel(pieces_ref, kernel_ref, down_ref, up_ref, out_ref):
    parts, rows, length = pieces_ref.shape
    share = rows // 2
    columns = jnp.concatenate(
        [pieces_ref[:, :share, :].reshape(length, length), pieces_ref[:, share:, :].reshape(length, length)],
        axis=0,
    )
    turned = product(pair(down_ref), split(columns))
    kernel = kernel_ref[...]
    turned = turned * jnp.concatenate([kernel, kernel], axis=0)
    out_ref[...] = product(pair(up_ref), split(turned)).reshape(parts, share, length)


def turn_kernel(pieces_ref, out_ref):
    share = math.isqrt(out_ref.shape[0] // 2)
    for part in range(2):
        for x in range(share):
            block = pieces_ref[pl.ds(part * share + x, share, stride=2 * share), :]
            out_ref[pl.ds((part * share + x) * share, share), :] = block


def all_columns(me, near_ref, far_ref, x):
    even = (me & 1) == 0
    tiles = []
    for part in range(2):
        for half in range(near_ref.shape[0]):
            slot = half ^ (me >> 1)
            near = near_ref[slot, part, x]
            far = far_ref[slot, part, x]
            tiles.append(jnp.where(even, near, far))
            tiles.append(jnp.where(even, far, near))
    return jnp.concatenate(tiles, axis=0)


def back(blocks, up_ref, down_ref, length):
    turned = product(pair(up_ref), split(blocks))
    rows = turned.shape[1] // length
    points = [parts_across(turned[:, x * length : (x + 1) * length]) for x in range(rows)]
    return product(split(jnp.concatenate(points, axis=0)), pair(down_ref))


def base_kernel(
    me_ref, energy_ref, near_ref, far_ref, orbital_ref, trial_ref, alda_ref, local_ref,
    up_ref, down_ref, out_ref,
):
    length = orbital_ref.shape[2]
    me = me_ref[0]
    energy = energy_ref[0]
    scale = 1.0 / float(length * length)
    rows = orbital_ref.shape[1]
    columns = [all_columns(me, near_ref, far_ref, x) for x in range(rows)]
    value = back(jnp.concatenate(columns, axis=1), up_ref, down_ref, length)
    for x in range(rows):
        factor = orbital_ref[0, x].astype(WIDE) * (alda_ref[x] * scale)
        weight = local_ref[x] - energy
        for k in range(2):
            block = value[x * length : (x + 1) * length, k * length : (k + 1) * length]
            out_ref[k, x] = block * factor + weight * trial_ref[k, 0, x].astype(WIDE)


def field_kernel(me_ref, *refs):
    *share_refs, orbital_ref, base_ref, up_ref, down_ref, out_ref, near_ref, far_ref = refs
    count = near_ref.shape[0]
    for i in range(count):
        near_ref[i] = share_refs[i][...]
    start = 0
    for ref in share_refs[count:]:
        far_ref[start : start + ref.shape[0]] = ref[...]
        start += ref.shape[0]
    length = orbital_ref.shape[2]
    parts = out_ref.shape[0]
    rows = orbital_ref.shape[1]
    columns = [all_columns(me_ref[0], near_ref, far_ref, x) for x in range(rows)]
    value = back(jnp.concatenate(columns, axis=1), up_ref, down_ref, length)
    fields = []
    for x in range(rows):
        orbital = orbital_ref[0, x].astype(WIDE)
        for k in range(2):
            block = value[x * length : (x + 1) * length, k * length : (k + 1) * length]
            fields.append(block * orbital + base_ref[k, x])
    table = (up_ref[0, :length, :], up_ref[1, :length, :])
    turned = product(split(jnp.concatenate(fields, axis=0)), table)
    for x in range(rows):
        points = swap_blocks(turned[2 * x * length : 2 * (x + 1) * length])
        waves = product(pair(down_ref), split(points))
        for k in range(2):
            for part in range(2):
                block = waves[part * length : (part + 1) * length, k * length : (k + 1) * length]
                out_ref[:, k, part, x] = block.reshape(parts, length // parts, length)


def final_kernel(pieces_ref, x_ref, real_ref, imag_ref):
    length = real_ref.shape[-1]
    share = real_ref.shape[2]
    table = pair(x_ref)
    for k in range(2):
        for b in range(share):
            parts = []
            for part in range(2):
                start = (k * 2 + part) * share * share + b
                block = pieces_ref[:, pl.ds(start, share, stride=share), :]
                parts.append(block.reshape(length, length))
            turned = product(split(jnp.concatenate(parts, axis=0).T), table)
            real_ref[k, 0, b] = turned[:, :length]
            imag_ref[k, 0, b] = turned[:, length:]


def signed(positions, length):
    return jnp.where(2 * positions < length, positions, positions - length).astype(WIDE)


def line_coulomb(b, length):
    a = lax.broadcasted_iota(jnp.int32, (length, length), 0)
    c = lax.broadcasted_iota(jnp.int32, (length, length), 1)
    squared = signed(a, length) ** 2 + signed(b, length) ** 2 + signed(c, length) ** 2
    scaled = box_length**2 / math.pi / jnp.maximum(squared, 1.0)
    return jnp.where(squared > 0, scaled, 0.0) / float(length**3)


def call(body, shapes, grant=GRANT, **options):
    return pl.pallas_call(
        body,
        out_shape=jax.tree.map(
            lambda s: jax.ShapeDtypeStruct(s, WIDE),
            shapes,
            is_leaf=lambda s: isinstance(s, tuple) and isinstance(s[0], int),
        ),
        compiler_params=pltpu.CompilerParams(vmem_limit_bytes=grant),
        **options,
    )


def exchange(array, axis):
    return lax.all_to_all(array, axis, split_axis=0, concat_axis=0, tiled=True)


def partner(array, mask):
    return lax.ppermute(array, "band", [(i, i ^ mask) for i in range(lax.axis_size("band"))])


def per_device(orbitals, trials, alda_kernel, local_potential, band_energies):
    length = orbitals.shape[2]
    parts = lax.axis_size("band")
    share = length // parts
    points = share * share
    tables = {name: jnp.asarray(table) for name, table in make_tables(length).items()}
    me = lax.axis_index("band")
    place = lax.axis_index("grid")
    copies = parts // share
    kernel = line_coulomb(me * share + place // copies, length)
    own_up = lax.dynamic_slice_in_dim(tables["up"], (place % copies) * length, length, 1)

    scalar = pl.BlockSpec(memory_space=pltpu.SMEM)
    orbital_block = pl.BlockSpec((1, ROWS, length, length), lambda i: (0, i, 0, 0))
    trial_block = pl.BlockSpec((2, 1, ROWS, length, length), lambda i: (0, 0, i, 0, 0))
    table_block = pl.BlockSpec((2, 2 * length, 2 * length), lambda i: (0, 0, 0))
    half_block = pl.BlockSpec((parts // 2, 2, ROWS, share, length), lambda i: (0, 0, i, 0, 0))
    local_block = pl.BlockSpec((ROWS, length, length), lambda i: (i, 0, 0))
    base_block = pl.BlockSpec((2, ROWS, length, length), lambda i: (0, i, 0, 0))
    steps = (share // ROWS,)

    held = pl.BlockSpec(memory_space=pltpu.HBM)
    half = share // 2
    some = (parts // 2, 2, half, share, length)
    kept, near, pieces = call(
        density_kernel,
        [some, some, (parts, 2, half, share, length)],
        grant=WIDE_GRANT,
        in_specs=[scalar] + [held] * 4,
        out_specs=[held] * 3,
        scratch_shapes=[
            pltpu.VMEM(orbitals.shape, NARROW),
            pltpu.VMEM(trials.shape, NARROW),
            pltpu.VMEM(tables["up"].shape, NARROW),
            pltpu.VMEM(tables["down"].shape, NARROW),
            pltpu.VMEM((2, *some), WIDE),
            pltpu.VMEM((parts, 2, half, share, length), WIDE),
            pltpu.SemaphoreType.DMA((2,)),
            pltpu.SemaphoreType.DMA((2, 2)),
            pltpu.SemaphoreType.DMA((3,)),
        ],
    )(me.reshape(1), orbitals, trials, tables["up"], tables["down"])
    near = partner(near.reshape(parts // 2, points, length), 1)
    near = near + kept.reshape(parts // 2, points, length)
    near = [near[0]] + [partner(near[i], 2 * i) for i in range(1, parts // 2)]
    pieces = exchange(pieces.reshape(parts, points, length), "band")
    spectrum, lines = call(
        share_kernel, [(2 * points, length), (parts, 2 * share, length)]
    )(pieces, *near)
    lines = exchange(lines, "grid")
    held = {0: spectrum}
    for mask in (2, 4, 8):
        held[mask] = partner(spectrum, mask)
    lines = call(line_kernel, (parts, share, length))(
        lines, kernel, tables["down"], own_up
    )
    lines, held[2], held[4], held[8] = lax.optimization_barrier((lines, held[2], held[4], held[8]))
    lines = exchange(lines, "grid").reshape(parts * share, length)
    both = partner(jnp.stack([held[4], held[8]]), 2)
    held[6], held[10] = both[0], both[1]
    held[12] = partner(held[8], 4)
    held[14] = partner(spectrum, 14)
    away = {}
    for masks in ((0, 2, 4, 8), (6, 10, 12, 14)):
        group = partner(jnp.stack([held[mask] for mask in masks]), 1)
        for i, mask in enumerate(masks):
            away[mask] = group[i]
    near = jnp.stack([held[mask] for mask in range(0, parts, 2)])
    far = jnp.stack([away[mask] for mask in range(0, parts, 2)])
    own = call(turn_kernel, (2 * points, length))(lines)
    gained = {0: own}
    for masks in ((2, 4, 6), (8, 10), (12, 14)):
        for mask in masks:
            gained[mask] = partner(own, mask)
    passed = [
        partner(jnp.stack([gained[mask] for mask in masks]), 1)
        for masks in ((0, 2, 4, 6), (8, 10), (12, 14))
    ]
    spread = [gained[mask].reshape(2, share, share, length) for mask in range(0, parts, 2)]
    spread += [array.reshape(-1, 2, share, share, length) for array in passed]
    base = call(
        base_kernel,
        (2, share, length, length),
        grid=steps,
        in_specs=[
            scalar, scalar, half_block, half_block, orbital_block, trial_block,
            local_block, local_block, table_block, table_block,
        ],
        out_specs=base_block,
    )(
        me.reshape(1),
        band_energies,
        near.reshape(parts // 2, 2, share, share, length),
        far.reshape(parts // 2, 2, share, share, length),
        orbitals,
        trials,
        alda_kernel,
        local_potential,
        tables["up"],
        tables["down"],
    )
    vector = pl.BlockSpec(memory_space=pltpu.VMEM)
    held = pltpu.VMEM((parts // 2, 2, share, share, length), WIDE)
    fields = call(
        field_kernel,
        (parts, 2, 2, share, share, length),
        in_specs=[scalar] + [vector] * (len(spread) + 4),
        scratch_shapes=[held, held],
    )(me.reshape(1), *spread, orbitals, base, tables["up"], tables["down"])
    received = exchange(fields.reshape(parts, 4 * points, length), "grid")
    shape = (2, 1, share, length, length)
    return tuple(call(final_kernel, [shape, shape])(received, tables["last"]))


def solution(mesh):
    placed = (
        P("band", "grid", None, None),
        P(None, "band", "grid", None, None),
        P("grid", None, None),
        P("grid", None, None),
        P("band"),
    )

    return jax.shard_map(
        per_device,
        mesh=mesh,
        in_specs=placed,
        out_specs=(P(None, "band", "grid", None, None), P(None, "band", "grid", None, None)),
        check_vma=False,
    )
```

profile of v0, /device:TPU:1, one launch (start us, length us, event | category | flops | bytes accessed | tf_op | source)
XLA Modules:
  0.0 161.3 jit_solution(13907280022867767388)
XLA Ops:
  0.6 4.2 %shard_map.95 = (f32[8,2,4,8,128]{4,3,2,1,0:T(8,128)}, f32[8,2,4,8,128]{4,3,2,1,0:T(8,128)}, f32[16,2,4,8,128]{4,3,2,1,0:T(8,128)}) custom-call(s32[1]{0:T(128)} %bitcast.me_ref, bf16[1,8,128,128]{3,2,1,0:T(8,128)(2,1)} %refs_11_.1, bf16[2,1,8,128,128]{4,3,2,1,0:T(8,128)(2,1)} %trial_ref.1, bf16[2,256,256]{2,1,0:T(8,128)(2,1)} %constant.61.clone.up_in.up_ref.refs_13_, ...), custom_call_target="tpu_custom_call" | custom-call | tf_op jit(solution)/shard_map/pallas_call | solution.py:324
  4.8 2.2 %collective-permute-start = (f32[8,64,128]{2,1,0:T(8,128)}, f32[8,64,128]{2,1,0:T(8,128)S(1)}, u32[]{:S(2)}, u32[]{:S(2)}) collective-permute-start(f32[8,64,128]{2,1,0:T(8,128)} %bitcast.96), channel_id=1, source_target_pairs={{0,16},{16,0},{32,48},{48,32},{64,80},{80,64},{96,112},{112,96},{1... | collective-permute-start | bytes 786440 | tf_op jit(solution)/shard_map/ppermute | solution.py:297
  7.0 8.3 %all-to-all-start = ((f32[16,64,128]{2,1,0:T(8,128)}), f32[16,64,128]{2,1,0:T(8,128)S(1)}, u32[]{:S(2)}, u32[]{:S(2)}) async-start(f32[16,64,128]{2,1,0:T(8,128)} %bitcast.87), calls=%async_computation | async-start | bytes 1048576 | tf_op jit(solution)/shard_map/all_to_all | solution.py:293
  16.4 3.4 %collective-permute-start.7 = (f32[64,128]{1,0:T(8,128)S(1)}, f32[64,128]{1,0:T(8,128)S(1)}, u32[]{:S(2)}, u32[]{:S(2)}) collective-permute-start(f32[64,128]{1,0:T(8,128)S(1)} %get-tuple-element.20), channel_id=1, source_target_pairs={{0,224},{16,240},{32,192},{48,208},{64,160},{80,176},{96,128},{112... | collective-permute-start | bytes 98312 | tf_op jit(solution)/shard_map/ppermute | solution.py:297
  21.1 3.3 %collective-permute-start.5 = (f32[64,128]{1,0:T(8,128)S(1)}, f32[64,128]{1,0:T(8,128)S(1)}, u32[]{:S(2)}, u32[]{:S(2)}) collective-permute-start(f32[64,128]{1,0:T(8,128)S(1)} %get-tuple-element.22), channel_id=1, source_target_pairs={{0,160},{16,176},{32,128},{48,144},{64,224},{80,240},{96,192},{112... | collective-permute-start | bytes 98312 | tf_op jit(solution)/shard_map/ppermute | solution.py:297
  25.6 2.0 %collective-permute-start.3 = (f32[64,128]{1,0:T(8,128)S(1)}, f32[64,128]{1,0:T(8,128)S(1)}, u32[]{:S(2)}, u32[]{:S(2)}) collective-permute-start(f32[64,128]{1,0:T(8,128)S(1)} %get-tuple-element.24), channel_id=1, source_target_pairs={{0,96},{16,112},{32,64},{48,80},{64,32},{80,48},{96,0},{112,16},{1... | collective-permute-start | bytes 98312 | tf_op jit(solution)/shard_map/ppermute | solution.py:297
  28.7 5.3 %collective-permute-start.2 = (f32[64,128]{1,0:T(8,128)S(1)}, f32[64,128]{1,0:T(8,128)S(1)}, u32[]{:S(2)}, u32[]{:S(2)}) collective-permute-start(f32[64,128]{1,0:T(8,128)S(1)} %get-tuple-element.25), channel_id=1, source_target_pairs={{0,64},{16,80},{32,96},{48,112},{64,0},{80,16},{96,32},{112,48},{1... | collective-permute-start | bytes 98312 | tf_op jit(solution)/shard_map/ppermute | solution.py:297
  34.0 3.8 %collective-permute-start.1 = (f32[64,128]{1,0:T(8,128)S(1)}, f32[64,128]{1,0:T(8,128)S(1)}, u32[]{:S(2)}, u32[]{:S(2)}) collective-permute-start(f32[64,128]{1,0:T(8,128)S(1)} %get-tuple-element.26), channel_id=1, source_target_pairs={{0,32},{16,48},{32,0},{48,16},{64,96},{80,112},{96,64},{112,80},{1... | collective-permute-start | bytes 98312 | tf_op jit(solution)/shard_map/ppermute | solution.py:297
  39.8 9.0 %all-to-all-start.1 = ((f32[16,16,128]{2,1,0:T(8,128)}), f32[16,16,128]{2,1,0:T(8,128)S(1)}, u32[]{:S(2)}, u32[]{:S(2)}) async-start(f32[16,16,128]{2,1,0:T(8,128)} %get-tuple-element.14), calls=%async_computation.1 | async-start | bytes 262144 | tf_op jit(solution)/shard_map/all_to_all | solution.py:293
  50.2 3.8 %collective-permute-start.10 = (f32[128,128]{1,0:T(8,128)S(1)}, f32[128,128]{1,0:T(8,128)S(1)}, u32[]{:S(2)}, u32[]{:S(2)}) collective-permute-start(f32[128,128]{1,0:T(8,128)S(1)} %get-tuple-element.15), channel_id=1, source_target_pairs={{0,128},{16,144},{32,160},{48,176},{64,192},{80,208},{96,224},{112... | collective-permute-start | bytes 196616 | tf_op jit(solution)/shard_map/ppermute | solution.py:297
  54.0 2.6 %collective-permute-start.9 = (f32[128,128]{1,0:T(8,128)S(1)}, f32[128,128]{1,0:T(8,128)S(1)}, u32[]{:S(2)}, u32[]{:S(2)}) collective-permute-start(f32[128,128]{1,0:T(8,128)S(1)} %get-tuple-element.15), channel_id=1, source_target_pairs={{0,64},{16,80},{32,96},{48,112},{64,0},{80,16},{96,32},{112,48},{1... | collective-permute-start | bytes 196616 | tf_op jit(solution)/shard_map/ppermute | solution.py:297
  59.4 1.9 %collective-permute-done.9 = f32[128,128]{1,0:T(8,128)S(1)} collective-permute-done((f32[128,128]{1,0:T(8,128)S(1)}, f32[128,128]{1,0:T(8,128)S(1)}, u32[]{:S(2)}, u32[]{:S(2)}) %collective-permute-start.9) | collective-permute-done | bytes 65568 | tf_op jit(solution)/shard_map/ppermute | solution.py:297
  61.3 9.0 %all-to-all-start.2 = ((f32[16,8,128]{2,1,0:T(8,128)}), f32[16,8,128]{2,1,0:T(8,128)S(1)}, u32[]{:S(2)}, u32[]{:S(2)}) async-start(f32[16,8,128]{2,1,0:T(8,128)} %shard_map.97), calls=%async_computation.2 | async-start | bytes 131072 | tf_op jit(solution)/shard_map/all_to_all | solution.py:293
  71.2 6.5 %all-to-all-done.2 = f32[16,8,128]{2,1,0:T(8,128)S(1)} async-done(((f32[16,8,128]{2,1,0:T(8,128)}), f32[16,8,128]{2,1,0:T(8,128)S(1)}, u32[]{:S(2)}, u32[]{:S(2)}) %all-to-all-start.2) | async-done | bytes 65568 | tf_op jit(solution)/shard_map/all_to_all | solution.py:293
  79.6 1.7 %collective-permute-start.11 = (f32[128,128]{1,0:T(8,128)S(1)}, f32[128,128]{1,0:T(8,128)S(1)}, u32[]{:S(2)}, u32[]{:S(2)}) collective-permute-start(f32[128,128]{1,0:T(8,128)S(1)} %shard_map.98), channel_id=1, source_target_pairs={{0,32},{16,48},{32,0},{48,16},{64,96},{80,112},{96,64},{112,80},{1... | collective-permute-start | bytes 196616 | tf_op jit(solution)/shard_map/ppermute | solution.py:297
  82.9 3.7 %collective-permute-done.12 = f32[128,128]{1,0:T(8,128)S(1)} collective-permute-done((f32[128,128]{1,0:T(8,128)S(1)}, f32[128,128]{1,0:T(8,128)S(1)}, u32[]{:S(2)}, u32[]{:S(2)}) %collective-permute-start.12) | collective-permute-done | bytes 65568 | tf_op jit(solution)/shard_map/ppermute | solution.py:297
  88.4 3.1 %collective-permute-done.17 = f32[128,128]{1,0:T(8,128)S(1)} collective-permute-done((f32[128,128]{1,0:T(8,128)S(1)}, f32[128,128]{1,0:T(8,128)S(1)}, u32[]{:S(2)}, u32[]{:S(2)}) %collective-permute-start.17) | collective-permute-done | bytes 65568 | tf_op jit(solution)/shard_map/ppermute | solution.py:297
  91.5 1.7 %collective-permute-start.15 = (f32[128,128]{1,0:T(8,128)S(1)}, f32[128,128]{1,0:T(8,128)S(1)}, u32[]{:S(2)}, u32[]{:S(2)}) collective-permute-start(f32[128,128]{1,0:T(8,128)S(1)} %shard_map.98), channel_id=1, source_target_pairs={{0,160},{16,176},{32,128},{48,144},{64,224},{80,240},{96,192},{112... | collective-permute-start | bytes 196616 | tf_op jit(solution)/shard_map/ppermute | solution.py:297
  93.1 2.9 %collective-permute-start.14 = (f32[128,128]{1,0:T(8,128)S(1)}, f32[128,128]{1,0:T(8,128)S(1)}, u32[]{:S(2)}, u32[]{:S(2)}) collective-permute-start(f32[128,128]{1,0:T(8,128)S(1)} %shard_map.98), channel_id=1, source_target_pairs={{0,128},{16,144},{32,160},{48,176},{64,192},{80,208},{96,224},{112... | collective-permute-start | bytes 196616 | tf_op jit(solution)/shard_map/ppermute | solution.py:297
  98.2 2.0 %collective-permute-done.14 = f32[128,128]{1,0:T(8,128)S(1)} collective-permute-done((f32[128,128]{1,0:T(8,128)S(1)}, f32[128,128]{1,0:T(8,128)S(1)}, u32[]{:S(2)}, u32[]{:S(2)}) %collective-permute-start.14) | collective-permute-done | bytes 65568 | tf_op jit(solution)/shard_map/ppermute | solution.py:297
  103.5 13.8 %collective-permute-done.25 = f32[4,128,128]{2,1,0:T(8,128)S(1)} collective-permute-done((f32[4,128,128]{2,1,0:T(8,128)S(1)}, f32[4,128,128]{2,1,0:T(8,128)S(1)}, u32[]{:S(2)}, u32[]{:S(2)}) %collective-permute-start.25) | collective-permute-done | bytes 262176 | tf_op jit(solution)/shard_map/ppermute | solution.py:297
  118.4 3.9 %shard_map.100 = f32[16,2,2,8,8,128]{5,4,3,2,1,0:T(8,128)S(1)} custom-call(s32[1]{0:T(128)} %bitcast.me_ref, f32[2,8,8,128]{3,2,1,0:T(8,128)S(1)} %bitcast.60, f32[2,8,8,128]{3,2,1,0:T(8,128)S(1)} %bitcast.74, f32[2,8,8,128]{3,2,1,0:T(8,128)S(1)} %bitcast.72, f32[2,8,8,128]{3,2,1,0:T(8,128)S(1)} %bitcast.70, f32[2,8,8,128]{3,2,1,0:T(8,128)S(1)} %bitcast.68, ...), custom_call_target="tpu_custom_call" | custom-call | tf_op jit(solution)/shard_map/pallas_call | solution.py:403
  122.3 36.6 %all_to_all.20.pieces_ref = f32[16,256,128]{2,1,0:T(8,128)S(1)} all-to-all(f32[16,256,128]{2,1,0:T(8,128)S(1)} %bitcast.57), channel_id=1, replica_groups=mesh['band'=16,'grid'=16] {'grid'}, dimensions={0} | all-to-all | bytes 4194304 | tf_op jit(solution)/shard_map/all_to_all | solution.py:293
  158.9 2.4 %shard_map.101 = (f32[2,1,8,128,128]{4,3,2,1,0:T(8,128)}, f32[2,1,8,128,128]{4,3,2,1,0:T(8,128)}) custom-call(f32[16,256,128]{2,1,0:T(8,128)S(1)} %all_to_all.20.pieces_ref, bf16[2,256,256]{2,1,0:T(8,128)(2,1)S(1)} %copy-done.6), custom_call_target="tpu_custom_call" | custom-call | tf_op jit(solution)/shard_map/pallas_call | solution.py:411
  (82 shorter events, 22.5 us)
Async XLA Ops:
  4.8 10.5 %collective-permute-start = (f32[8,64,128]{2,1,0:T(8,128)}, f32[8,64,128]{2,1,0:T(8,128)S(1)}, u32[]{:S(2)}, u32[]{:S(2)}) collective-permute-start(f32[8,64,128]{2,1,0:T(8,128)} %bitcast.96), channel_id=1, source_target_pairs={{0,16},{16,0},{32,48},{48,32},{64,80},{80,64},{96,112},{112,96},{1... | collective-permute-start | bytes 786440 | tf_op jit(solution)/shard_map/ppermute | solution.py:297
  7.0 32.1 %all-to-all-start = ((f32[16,64,128]{2,1,0:T(8,128)}), f32[16,64,128]{2,1,0:T(8,128)S(1)}, u32[]{:S(2)}, u32[]{:S(2)}) async-start(f32[16,64,128]{2,1,0:T(8,128)} %bitcast.87), calls=%async_computation | async-start | bytes 1048576 | tf_op jit(solution)/shard_map/all_to_all | solution.py:293
  16.4 12.3 %collective-permute-start.7 = (f32[64,128]{1,0:T(8,128)S(1)}, f32[64,128]{1,0:T(8,128)S(1)}, u32[]{:S(2)}, u32[]{:S(2)}) collective-permute-start(f32[64,128]{1,0:T(8,128)S(1)} %get-tuple-element.20), channel_id=1, source_target_pairs={{0,224},{16,240},{32,192},{48,208},{64,160},{80,176},{96,128},{112... | collective-permute-start | bytes 98312 | tf_op jit(solution)/shard_map/ppermute | solution.py:297
  19.8 14.2 %collective-permute-start.6 = (f32[64,128]{1,0:T(8,128)S(1)}, f32[64,128]{1,0:T(8,128)S(1)}, u32[]{:S(2)}, u32[]{:S(2)}) collective-permute-start(f32[64,128]{1,0:T(8,128)S(1)} %get-tuple-element.21), channel_id=1, source_target_pairs={{0,192},{16,208},{32,224},{48,240},{64,128},{80,144},{96,160},{112... | collective-permute-start | bytes 98312 | tf_op jit(solution)/shard_map/ppermute | solution.py:297
  21.1 16.9 %collective-permute-start.5 = (f32[64,128]{1,0:T(8,128)S(1)}, f32[64,128]{1,0:T(8,128)S(1)}, u32[]{:S(2)}, u32[]{:S(2)}) collective-permute-start(f32[64,128]{1,0:T(8,128)S(1)} %get-tuple-element.22), channel_id=1, source_target_pairs={{0,160},{16,176},{32,128},{48,144},{64,224},{80,240},{96,192},{112... | collective-permute-start | bytes 98312 | tf_op jit(solution)/shard_map/ppermute | solution.py:297
  24.4 13.6 %collective-permute-start.4 = (f32[64,128]{1,0:T(8,128)S(1)}, f32[64,128]{1,0:T(8,128)S(1)}, u32[]{:S(2)}, u32[]{:S(2)}) collective-permute-start(f32[64,128]{1,0:T(8,128)S(1)} %get-tuple-element.23), channel_id=1, source_target_pairs={{0,128},{16,144},{32,160},{48,176},{64,192},{80,208},{96,224},{112... | collective-permute-start | bytes 98312 | tf_op jit(solution)/shard_map/ppermute | solution.py:297
  25.6 12.4 %collective-permute-start.3 = (f32[64,128]{1,0:T(8,128)S(1)}, f32[64,128]{1,0:T(8,128)S(1)}, u32[]{:S(2)}, u32[]{:S(2)}) collective-permute-start(f32[64,128]{1,0:T(8,128)S(1)} %get-tuple-element.24), channel_id=1, source_target_pairs={{0,96},{16,112},{32,64},{48,80},{64,32},{80,48},{96,0},{112,16},{1... | collective-permute-start | bytes 98312 | tf_op jit(solution)/shard_map/ppermute | solution.py:297
  28.7 9.3 %collective-permute-start.2 = (f32[64,128]{1,0:T(8,128)S(1)}, f32[64,128]{1,0:T(8,128)S(1)}, u32[]{:S(2)}, u32[]{:S(2)}) collective-permute-start(f32[64,128]{1,0:T(8,128)S(1)} %get-tuple-element.25), channel_id=1, source_target_pairs={{0,64},{16,80},{32,96},{48,112},{64,0},{80,16},{96,32},{112,48},{1... | collective-permute-start | bytes 98312 | tf_op jit(solution)/shard_map/ppermute | solution.py:297
  39.8 16.8 %all-to-all-start.1 = ((f32[16,16,128]{2,1,0:T(8,128)}), f32[16,16,128]{2,1,0:T(8,128)S(1)}, u32[]{:S(2)}, u32[]{:S(2)}) async-start(f32[16,16,128]{2,1,0:T(8,128)} %get-tuple-element.14), calls=%async_computation.1 | async-start | bytes 262144 | tf_op jit(solution)/shard_map/all_to_all | solution.py:293
  49.6 51.4 %collective-permute-start.23 = (f32[128,128]{1,0:T(8,128)S(1)}, f32[128,128]{1,0:T(8,128)S(1)}, u32[]{:S(2)}, u32[]{:S(2)}) collective-permute-start(f32[128,128]{1,0:T(8,128)S(1)} %get-tuple-element.15), channel_id=1, source_target_pairs={{0,224},{16,240},{32,192},{48,208},{64,160},{80,176},{96,128},{112... | collective-permute-start | bytes 196616 | tf_op jit(solution)/shard_map/ppermute | solution.py:297
  50.2 9.2 %collective-permute-start.10 = (f32[128,128]{1,0:T(8,128)S(1)}, f32[128,128]{1,0:T(8,128)S(1)}, u32[]{:S(2)}, u32[]{:S(2)}) collective-permute-start(f32[128,128]{1,0:T(8,128)S(1)} %get-tuple-element.15), channel_id=1, source_target_pairs={{0,128},{16,144},{32,160},{48,176},{64,192},{80,208},{96,224},{112... | collective-permute-start | bytes 196616 | tf_op jit(solution)/shard_map/ppermute | solution.py:297
  54.0 7.3 %collective-permute-start.9 = (f32[128,128]{1,0:T(8,128)S(1)}, f32[128,128]{1,0:T(8,128)S(1)}, u32[]{:S(2)}, u32[]{:S(2)}) collective-permute-start(f32[128,128]{1,0:T(8,128)S(1)} %get-tuple-element.15), channel_id=1, source_target_pairs={{0,64},{16,80},{32,96},{48,112},{64,0},{80,16},{96,32},{112,48},{1... | collective-permute-start | bytes 196616 | tf_op jit(solution)/shard_map/ppermute | solution.py:297
  61.3 16.4 %all-to-all-start.2 = ((f32[16,8,128]{2,1,0:T(8,128)}), f32[16,8,128]{2,1,0:T(8,128)S(1)}, u32[]{:S(2)}, u32[]{:S(2)}) async-start(f32[16,8,128]{2,1,0:T(8,128)} %shard_map.97), calls=%async_computation.2 | async-start | bytes 131072 | tf_op jit(solution)/shard_map/all_to_all | solution.py:293
  70.3 31.5 %collective-permute-start.22 = (f32[128,128]{1,0:T(8,128)S(1)}, f32[128,128]{1,0:T(8,128)S(1)}, u32[]{:S(2)}, u32[]{:S(2)}) collective-permute-start(f32[128,128]{1,0:T(8,128)S(1)} %collective-permute-done.10), channel_id=1, source_target_pairs={{0,64},{16,80},{32,96},{48,112},{64,0},{80,16},{96,32},{112,48},{1... | collective-permute-start | bytes 196616 | tf_op jit(solution)/shard_map/ppermute | solution.py:297
  79.1 7.4 %collective-permute-start.12 = (f32[128,128]{1,0:T(8,128)S(1)}, f32[128,128]{1,0:T(8,128)S(1)}, u32[]{:S(2)}, u32[]{:S(2)}) collective-permute-start(f32[128,128]{1,0:T(8,128)S(1)} %shard_map.98), channel_id=1, source_target_pairs={{0,64},{16,80},{32,96},{48,112},{64,0},{80,16},{96,32},{112,48},{1... | collective-permute-start | bytes 196616 | tf_op jit(solution)/shard_map/ppermute | solution.py:297
  79.6 7.7 %collective-permute-start.11 = (f32[128,128]{1,0:T(8,128)S(1)}, f32[128,128]{1,0:T(8,128)S(1)}, u32[]{:S(2)}, u32[]{:S(2)}) collective-permute-start(f32[128,128]{1,0:T(8,128)S(1)} %shard_map.98), channel_id=1, source_target_pairs={{0,32},{16,48},{32,0},{48,16},{64,96},{80,112},{96,64},{112,80},{1... | collective-permute-start | bytes 196616 | tf_op jit(solution)/shard_map/ppermute | solution.py:297
  82.8 19.7 %collective-permute-start.21 = (f32[2,128,128]{2,1,0:T(8,128)S(1)}, f32[2,128,128]{2,1,0:T(8,128)S(1)}, u32[]{:S(2)}, u32[]{:S(2)}) collective-permute-start(f32[2,128,128]{2,1,0:T(8,128)S(1)} %pad_maximum_fusion.6), channel_id=1, source_target_pairs={{0,32},{16,48},{32,0},{48,16},{64,96},{80,112},{96,64},{112,80},{1... | collective-permute-start | bytes 393224 | tf_op jit(solution)/shard_map/ppermute | solution.py:297
  91.5 6.1 %collective-permute-start.15 = (f32[128,128]{1,0:T(8,128)S(1)}, f32[128,128]{1,0:T(8,128)S(1)}, u32[]{:S(2)}, u32[]{:S(2)}) collective-permute-start(f32[128,128]{1,0:T(8,128)S(1)} %shard_map.98), channel_id=1, source_target_pairs={{0,160},{16,176},{32,128},{48,144},{64,224},{80,240},{96,192},{112... | collective-permute-start | bytes 196616 | tf_op jit(solution)/shard_map/ppermute | solution.py:297
  93.1 7.0 %collective-permute-start.14 = (f32[128,128]{1,0:T(8,128)S(1)}, f32[128,128]{1,0:T(8,128)S(1)}, u32[]{:S(2)}, u32[]{:S(2)}) collective-permute-start(f32[128,128]{1,0:T(8,128)S(1)} %shard_map.98), channel_id=1, source_target_pairs={{0,128},{16,144},{32,160},{48,176},{64,192},{80,208},{96,224},{112... | collective-permute-start | bytes 196616 | tf_op jit(solution)/shard_map/ppermute | solution.py:297
  97.6 5.8 %collective-permute-start.24 = (f32[4,128,128]{2,1,0:T(8,128)S(1)}, f32[4,128,128]{2,1,0:T(8,128)S(1)}, u32[]{:S(2)}, u32[]{:S(2)}) collective-permute-start(f32[4,128,128]{2,1,0:T(8,128)S(1)} %pad_maximum_fusion.2), channel_id=1, source_target_pairs={{0,16},{16,0},{32,48},{48,32},{64,80},{80,64},{96,112},{112,96},{1... | collective-permute-start | bytes 786440 | tf_op jit(solution)/shard_map/ppermute | solution.py:297
  100.2 18.2 %collective-permute-start.20 = (f32[2,128,128]{2,1,0:T(8,128)S(1)}, f32[2,128,128]{2,1,0:T(8,128)S(1)}, u32[]{:S(2)}, u32[]{:S(2)}) collective-permute-start(f32[2,128,128]{2,1,0:T(8,128)S(1)} %pad_maximum_fusion.5), channel_id=1, source_target_pairs={{0,16},{16,0},{32,48},{48,32},{64,80},{80,64},{96,112},{112,96},{1... | collective-permute-start | bytes 393224 | tf_op jit(solution)/shard_map/ppermute | solution.py:297
  101.0 17.4 %collective-permute-start.19 = (f32[2,128,128]{2,1,0:T(8,128)S(1)}, f32[2,128,128]{2,1,0:T(8,128)S(1)}, u32[]{:S(2)}, u32[]{:S(2)}) collective-permute-start(f32[2,128,128]{2,1,0:T(8,128)S(1)} %pad_maximum_fusion.4), channel_id=1, source_target_pairs={{0,16},{16,0},{32,48},{48,32},{64,80},{80,64},{96,112},{112,96},{1... | collective-permute-start | bytes 393224 | tf_op jit(solution)/shard_map/ppermute | solution.py:297
  101.7 16.7 %collective-permute-start.18 = (f32[4,128,128]{2,1,0:T(8,128)S(1)}, f32[4,128,128]{2,1,0:T(8,128)S(1)}, u32[]{:S(2)}, u32[]{:S(2)}) collective-permute-start(f32[4,128,128]{2,1,0:T(8,128)S(1)} %pad_maximum_fusion.1), channel_id=1, source_target_pairs={{0,16},{16,0},{32,48},{48,32},{64,80},{80,64},{96,112},{112,96},{1... | collective-permute-start | bytes 786440 | tf_op jit(solution)/shard_map/ppermute | solution.py:297
  102.6 14.6 %collective-permute-start.25 = (f32[4,128,128]{2,1,0:T(8,128)S(1)}, f32[4,128,128]{2,1,0:T(8,128)S(1)}, u32[]{:S(2)}, u32[]{:S(2)}) collective-permute-start(f32[4,128,128]{2,1,0:T(8,128)S(1)} %pad_maximum_fusion.3), channel_id=1, source_target_pairs={{0,16},{16,0},{32,48},{48,32},{64,80},{80,64},{96,112},{112,96},{1... | collective-permute-start | bytes 786440 | tf_op jit(solution)/shard_map/ppermute | solution.py:297
  (12 other events, 274.0 us)
where the time goes:
time: 163 us; the launch traced here: 161 us
  starting transfers between devices  70.4 us (43%)
  waiting for transfers between devices  37.9 us (23%)
  blocking collectives  36.6 us (22%)
  Pallas kernels  13.3 us (8%)
  between operations  1.68 us (1%)
    ppermute x26, starting transfers between devices, partner(): lax.ppermute(array, 'band', [(i, i ^ mask) for i in range(lax.axis_size('...  44.1 us
    all_to_all x1, blocking collectives, exchange(): return lax.all_to_all(array, axis, split_axis=0, concat_axis=0, tiled=True)  36.6 us
    ppermute x26, waiting for transfers between devices, partner(): lax.ppermute(array, 'band', [(i, i ^ mask) for i in range(lax.axis_size('...  31.4 us
    all_to_all x3, starting transfers between devices, exchange(): return lax.all_to_all(array, axis, split_axis=0, concat_axis=0, tiled=True)  26.4 us
    all_to_all x3, waiting for transfers between devices, exchange(): return lax.all_to_all(array, axis, split_axis=0, concat_axis=0, tiled=True)  6.5 us
    pallas_call x1, Pallas kernels, per_device(): call(density_kernel, [some, some, (parts, 2, half, share, length)], grant...  4.17 us
    pallas_call x1, Pallas kernels, per_device(): call(field_kernel, (parts, 2, 2, share, share, length), in_specs=[scalar]...  3.87 us
  transfers between devices with their start and end apart: 29, of which 11 were waited for; matrix products, arithmetic and copies ran while one was open for 1% of the time, Pallas kernels for 1%

commit v1 on v0

--- a/solution.py
+++ b/solution.py
@@ -170,12 +170,19 @@
     out_ref[...] = product(pair(up_ref), split(turned)).reshape(parts, share, length)
 
 
-def turn_kernel(pieces_ref, out_ref):
-    share = math.isqrt(out_ref.shape[0] // 2)
+def spread_kernel(pieces_ref, out_ref, own_ref):
+    parts, _, _ = out_ref.shape
+    share = pieces_ref.shape[0] // parts
+    half = share // 2
     for part in range(2):
         for x in range(share):
             block = pieces_ref[pl.ds(part * share + x, share, stride=2 * share), :]
-            out_ref[pl.ds((part * share + x) * share, share), :] = block
+            rows = pl.ds((part * half + x % half) * share, share)
+            if x >= half:
+                own_ref[rows, :] = block
+                continue
+            for i in range(parts):
+                out_ref[i, rows, :] = block
 
 
 def all_columns(me, near_ref, far_ref, x):
@@ -217,8 +224,11 @@
             out_ref[k, x] = block * factor + weight * trial_ref[k, 0, x].astype(WIDE)
 
 
-def field_kernel(me_ref, *refs):
+def field_kernel(me_ref, potential_ref, *refs):
     *share_refs, orbital_ref, base_ref, up_ref, down_ref, out_ref, near_ref, far_ref = refs
+    length = orbital_ref.shape[2]
+    parts = potential_ref.shape[0]
+    rows = orbital_ref.shape[1]
     count = near_ref.shape[0]
     for i in range(count):
         near_ref[i] = share_refs[i][...]
@@ -226,10 +236,14 @@
     for ref in share_refs[count:]:
         far_ref[start : start + ref.shape[0]] = ref[...]
         start += ref.shape[0]
-    length = orbital_ref.shape[2]
-    parts = out_ref.shape[0]
-    rows = orbital_ref.shape[1]
-    columns = [all_columns(me_ref[0], near_ref, far_ref, x) for x in range(rows)]
+    columns = []
+    for x in range(rows // 2):
+        columns.append(
+            jnp.concatenate(
+                [potential_ref[:, part, x].reshape(length, length) for part in range(2)], axis=0
+            )
+        )
+    columns += [all_columns(me_ref[0], near_ref, far_ref, x) for x in range(rows // 2)]
     value = back(jnp.concatenate(columns, axis=1), up_ref, down_ref, length)
     fields = []
     for x in range(rows):
@@ -353,7 +367,7 @@
     lines = call(line_kernel, (parts, share, length))(
         lines, kernel, tables["down"], own_up
     )
-    lines, held[2], held[4], held[8] = lax.optimization_barrier((lines, held[2], held[4], held[8]))
+    _, held[2], held[4], held[8] = lax.optimization_barrier((lines, held[2], held[4], held[8]))
     lines = exchange(lines, "grid").reshape(parts * share, length)
     both = partner(jnp.stack([held[4], held[8]]), 2)
     held[6], held[10] = both[0], both[1]
@@ -366,17 +380,20 @@
             away[mask] = group[i]
     near = jnp.stack([held[mask] for mask in range(0, parts, 2)])
     far = jnp.stack([away[mask] for mask in range(0, parts, 2)])
-    own = call(turn_kernel, (2 * points, length))(lines)
+    potential, own = call(spread_kernel, [(parts, points, length), (points, length)])(lines)
+    potential = exchange(potential, "band").reshape(
+        parts, 2, half, share, length
+    )
     gained = {0: own}
-    for masks in ((2, 4, 6), (8, 10), (12, 14)):
+    for masks in ((2, 4, 6), (8, 10, 12, 14)):
         for mask in masks:
             gained[mask] = partner(own, mask)
     passed = [
         partner(jnp.stack([gained[mask] for mask in masks]), 1)
-        for masks in ((0, 2, 4, 6), (8, 10), (12, 14))
+        for masks in ((0, 2, 4, 6), (8, 10, 12, 14))
     ]
-    spread = [gained[mask].reshape(2, share, share, length) for mask in range(0, parts, 2)]
-    spread += [array.reshape(-1, 2, share, share, length) for array in passed]
+    spread = [gained[mask].reshape(2, half, share, length) for mask in range(0, parts, 2)]
+    spread += [array.reshape(-1, 2, half, share, length) for array in passed]
     base = call(
         base_kernel,
         (2, share, length, length),
@@ -399,13 +416,13 @@
         tables["down"],
     )
     vector = pl.BlockSpec(memory_space=pltpu.VMEM)
-    held = pltpu.VMEM((parts // 2, 2, share, share, length), WIDE)
+    shares = pltpu.VMEM(some, WIDE)
     fields = call(
         field_kernel,
         (parts, 2, 2, share, share, length),
-        in_specs=[scalar] + [vector] * (len(spread) + 4),
-        scratch_shapes=[held, held],
-    )(me.reshape(1), *spread, orbitals, base, tables["up"], tables["down"])
+        in_specs=[scalar] + [vector] * (len(spread) + 5),
+        scratch_shapes=[shares, shares],
+    )(me.reshape(1), potential, *spread, orbitals, base, tables["up"], tables["down"])
     received = exchange(fields.reshape(parts, 4 * points, length), "grid")
     shape = (2, 1, share, length, length)
     return tuple(call(final_kernel, [shape, shape])(received, tables["last"]))

time: 163 us -> 163 us (level)
  waiting for transfers between devices: 37.9 us -> 31.5 us
  starting transfers between devices: 70.4 us -> 76.7 us
    ppermute x26 -> x25, waiting for transfers between devices: 31.4 us -> 24.2 us  [partner(): lax.ppermute(array, 'band', [(i, i ^ mask) for i in range(lax.axis_size('...]
    all_to_all x3 -> x4, starting transfers between devices: 26.4 us -> 30.1 us  [exchange(): return lax.all_to_all(array, axis, split_axis=0, concat_axis=0, tiled=True)]
    ppermute x26 -> x25, starting transfers between devices: 44.1 us -> 46.6 us  [partner(): lax.ppermute(array, 'band', [(i, i ^ mask) for i in range(lax.axis_size('...]
    all_to_all x3 -> x4, waiting for transfers between devices: 6.5 us -> 7.29 us  [exchange(): return lax.all_to_all(array, axis, split_axis=0, concat_axis=0, tiled=True)]
  transfers between devices with their start and end apart: 29 -> 29, of which waited for: 11 -> 6; matrix products, arithmetic and copies ran while one was open for 1% -> 1% of each run, Pallas kernels for 1% -> 2%
where the time goes in v1:
time: 163 us; the launch traced here: 162 us
  starting transfers between devices  76.7 us (47%)
  blocking collectives  36.6 us (22%)
  waiting for transfers between devices  31.5 us (19%)
  Pallas kernels  14.1 us (9%)
  between operations  1.71 us (1%)
    ppermute x25, starting transfers between devices, partner(): lax.ppermute(array, 'band', [(i, i ^ mask) for i in range(lax.axis_size('...  46.6 us
    all_to_all x1, blocking collectives, exchange(): return lax.all_to_all(array, axis, split_axis=0, concat_axis=0, tiled=True)  36.6 us
    all_to_all x4, starting transfers between devices, exchange(): return lax.all_to_all(array, axis, split_axis=0, concat_axis=0, tiled=True)  30.1 us
    ppermute x25, waiting for transfers between devices, partner(): lax.ppermute(array, 'band', [(i, i ^ mask) for i in range(lax.axis_size('...  24.2 us
    all_to_all x4, waiting for transfers between devices, exchange(): return lax.all_to_all(array, axis, split_axis=0, concat_axis=0, tiled=True)  7.29 us
    pallas_call x1, Pallas kernels, per_device(): call(density_kernel, [some, some, (parts, 2, half, share, length)], grant...  4.17 us
    pallas_call x1, Pallas kernels, per_device(): call(field_kernel, (parts, 2, 2, share, share, length), in_specs=[scalar]...  3.81 us
  transfers between devices with their start and end apart: 29, of which 6 were waited for; matrix products, arithmetic and copies ran while one was open for 1% of the time, Pallas kernels for 2%

profile of v1, /device:TPU:1, one launch (start us, length us, event | category | flops | bytes accessed | tf_op | source)
XLA Modules:
  0.0 162.0 jit_solution(7034110418734141341)
XLA Ops:
  0.6 4.2 %shard_map.95 = (f32[8,2,4,8,128]{4,3,2,1,0:T(8,128)}, f32[8,2,4,8,128]{4,3,2,1,0:T(8,128)}, f32[16,2,4,8,128]{4,3,2,1,0:T(8,128)}) custom-call(s32[1]{0:T(128)} %bitcast.me_ref, bf16[1,8,128,128]{3,2,1,0:T(8,128)(2,1)} %refs_10_.1, bf16[2,1,8,128,128]{4,3,2,1,0:T(8,128)(2,1)} %trial_ref.1, bf16[2,256,256]{2,1,0:T(8,128)(2,1)} %constant.61.clone.up_in.up_ref.refs_12_, ...), custom_call_target="tpu_custom_call" | custom-call | tf_op jit(solution)/shard_map/pallas_call | solution.py:338
  4.8 2.2 %collective-permute-start = (f32[8,64,128]{2,1,0:T(8,128)}, f32[8,64,128]{2,1,0:T(8,128)S(1)}, u32[]{:S(2)}, u32[]{:S(2)}) collective-permute-start(f32[8,64,128]{2,1,0:T(8,128)} %bitcast.96), channel_id=1, source_target_pairs={{0,16},{16,0},{32,48},{48,32},{64,80},{80,64},{96,112},{112,96},{1... | collective-permute-start | bytes 786440 | tf_op jit(solution)/shard_map/ppermute | solution.py:311
  7.0 8.3 %all-to-all-start = ((f32[16,64,128]{2,1,0:T(8,128)}), f32[16,64,128]{2,1,0:T(8,128)S(1)}, u32[]{:S(2)}, u32[]{:S(2)}) async-start(f32[16,64,128]{2,1,0:T(8,128)} %bitcast.87), calls=%async_computation | async-start | bytes 1048576 | tf_op jit(solution)/shard_map/all_to_all | solution.py:307
  16.4 3.4 %collective-permute-start.7 = (f32[64,128]{1,0:T(8,128)S(1)}, f32[64,128]{1,0:T(8,128)S(1)}, u32[]{:S(2)}, u32[]{:S(2)}) collective-permute-start(f32[64,128]{1,0:T(8,128)S(1)} %get-tuple-element.22), channel_id=1, source_target_pairs={{0,224},{16,240},{32,192},{48,208},{64,160},{80,176},{96,128},{112... | collective-permute-start | bytes 98312 | tf_op jit(solution)/shard_map/ppermute | solution.py:311
  21.1 3.3 %collective-permute-start.5 = (f32[64,128]{1,0:T(8,128)S(1)}, f32[64,128]{1,0:T(8,128)S(1)}, u32[]{:S(2)}, u32[]{:S(2)}) collective-permute-start(f32[64,128]{1,0:T(8,128)S(1)} %get-tuple-element.24), channel_id=1, source_target_pairs={{0,160},{16,176},{32,128},{48,144},{64,224},{80,240},{96,192},{112... | collective-permute-start | bytes 98312 | tf_op jit(solution)/shard_map/ppermute | solution.py:311
  25.6 2.0 %collective-permute-start.3 = (f32[64,128]{1,0:T(8,128)S(1)}, f32[64,128]{1,0:T(8,128)S(1)}, u32[]{:S(2)}, u32[]{:S(2)}) collective-permute-start(f32[64,128]{1,0:T(8,128)S(1)} %get-tuple-element.26), channel_id=1, source_target_pairs={{0,96},{16,112},{32,64},{48,80},{64,32},{80,48},{96,0},{112,16},{1... | collective-permute-start | bytes 98312 | tf_op jit(solution)/shard_map/ppermute | solution.py:311
  28.7 5.3 %collective-permute-start.2 = (f32[64,128]{1,0:T(8,128)S(1)}, f32[64,128]{1,0:T(8,128)S(1)}, u32[]{:S(2)}, u32[]{:S(2)}) collective-permute-start(f32[64,128]{1,0:T(8,128)S(1)} %get-tuple-element.27), channel_id=1, source_target_pairs={{0,64},{16,80},{32,96},{48,112},{64,0},{80,16},{96,32},{112,48},{1... | collective-permute-start | bytes 98312 | tf_op jit(solution)/shard_map/ppermute | solution.py:311
  34.0 3.8 %collective-permute-start.1 = (f32[64,128]{1,0:T(8,128)S(1)}, f32[64,128]{1,0:T(8,128)S(1)}, u32[]{:S(2)}, u32[]{:S(2)}) collective-permute-start(f32[64,128]{1,0:T(8,128)S(1)} %get-tuple-element.28), channel_id=1, source_target_pairs={{0,32},{16,48},{32,0},{48,16},{64,96},{80,112},{96,64},{112,80},{1... | collective-permute-start | bytes 98312 | tf_op jit(solution)/shard_map/ppermute | solution.py:311
  39.8 9.0 %all-to-all-start.1 = ((f32[16,16,128]{2,1,0:T(8,128)}), f32[16,16,128]{2,1,0:T(8,128)S(1)}, u32[]{:S(2)}, u32[]{:S(2)}) async-start(f32[16,16,128]{2,1,0:T(8,128)} %get-tuple-element.15), calls=%async_computation.1 | async-start | bytes 262144 | tf_op jit(solution)/shard_map/all_to_all | solution.py:307
  50.2 3.8 %collective-permute-start.19 = (f32[128,128]{1,0:T(8,128)S(1)}, f32[128,128]{1,0:T(8,128)S(1)}, u32[]{:S(2)}, u32[]{:S(2)}) collective-permute-start(f32[128,128]{1,0:T(8,128)S(1)} %get-tuple-element.18), channel_id=1, source_target_pairs={{0,128},{16,144},{32,160},{48,176},{64,192},{80,208},{96,224},{112... | collective-permute-start | bytes 196616 | tf_op jit(solution)/shard_map/ppermute | solution.py:311
  54.0 2.6 %collective-permute-start.18 = (f32[128,128]{1,0:T(8,128)S(1)}, f32[128,128]{1,0:T(8,128)S(1)}, u32[]{:S(2)}, u32[]{:S(2)}) collective-permute-start(f32[128,128]{1,0:T(8,128)S(1)} %get-tuple-element.18), channel_id=1, source_target_pairs={{0,64},{16,80},{32,96},{48,112},{64,0},{80,16},{96,32},{112,48},{1... | collective-permute-start | bytes 196616 | tf_op jit(solution)/shard_map/ppermute | solution.py:311
  57.7 8.1 %all-to-all-start.2 = ((f32[16,8,128]{2,1,0:T(8,128)}), f32[16,8,128]{2,1,0:T(8,128)S(1)}, u32[]{:S(2)}, u32[]{:S(2)}) async-start(f32[16,8,128]{2,1,0:T(8,128)} %shard_map.97), calls=%async_computation.2 | async-start | bytes 131072 | tf_op jit(solution)/shard_map/all_to_all | solution.py:307
  65.9 7.3 %all-to-all-done.2 = f32[16,8,128]{2,1,0:T(8,128)S(1)} async-done(((f32[16,8,128]{2,1,0:T(8,128)}), f32[16,8,128]{2,1,0:T(8,128)S(1)}, u32[]{:S(2)}, u32[]{:S(2)}) %all-to-all-start.2) | async-done | bytes 65568 | tf_op jit(solution)/shard_map/all_to_all | solution.py:307
  74.7 4.3 %collective-permute-start.13 = (f32[64,128]{1,0:T(8,128)S(1)}, f32[64,128]{1,0:T(8,128)S(1)}, u32[]{:S(2)}, u32[]{:S(2)}) collective-permute-start(f32[64,128]{1,0:T(8,128)S(1)} %get-tuple-element.17), channel_id=1, source_target_pairs={{0,192},{16,208},{32,224},{48,240},{64,128},{80,144},{96,160},{112... | collective-permute-start | bytes 98312 | tf_op jit(solution)/shard_map/ppermute | solution.py:311
  79.2 2.9 %collective-permute-start.11 = (f32[64,128]{1,0:T(8,128)S(1)}, f32[64,128]{1,0:T(8,128)S(1)}, u32[]{:S(2)}, u32[]{:S(2)}) collective-permute-start(f32[64,128]{1,0:T(8,128)S(1)} %get-tuple-element.17), channel_id=1, source_target_pairs={{0,128},{16,144},{32,160},{48,176},{64,192},{80,208},{96,224},{112... | collective-permute-start | bytes 98312 | tf_op jit(solution)/shard_map/ppermute | solution.py:311
  82.1 4.7 %all-to-all-start.3 = ((f32[16,64,128]{2,1,0:T(8,128)}), f32[16,64,128]{2,1,0:T(8,128)S(1)}, u32[]{:S(2)}, u32[]{:S(2)}) async-start(f32[16,64,128]{2,1,0:T(8,128)} %get-tuple-element.16), calls=%async_computation.3 | async-start | bytes 1048576 | tf_op jit(solution)/shard_map/all_to_all | solution.py:307
  86.8 1.7 %collective-permute-start.20 = (f32[2,128,128]{2,1,0:T(8,128)S(1)}, f32[2,128,128]{2,1,0:T(8,128)S(1)}, u32[]{:S(2)}, u32[]{:S(2)}) collective-permute-start(f32[2,128,128]{2,1,0:T(8,128)S(1)} %pad_maximum_fusion.5), channel_id=1, source_target_pairs={{0,32},{16,48},{32,0},{48,16},{64,96},{80,112},{96,64},{112,80},{1... | collective-permute-start | bytes 393224 | tf_op jit(solution)/shard_map/ppermute | solution.py:311
  88.5 2.1 %collective-permute-start.10 = (f32[64,128]{1,0:T(8,128)S(1)}, f32[64,128]{1,0:T(8,128)S(1)}, u32[]{:S(2)}, u32[]{:S(2)}) collective-permute-start(f32[64,128]{1,0:T(8,128)S(1)} %get-tuple-element.17), channel_id=1, source_target_pairs={{0,96},{16,112},{32,64},{48,80},{64,32},{80,48},{96,0},{112,16},{1... | collective-permute-start | bytes 98312 | tf_op jit(solution)/shard_map/ppermute | solution.py:311
  92.1 11.4 %collective-permute-done.10 = f32[64,128]{1,0:T(8,128)S(1)} collective-permute-done((f32[64,128]{1,0:T(8,128)S(1)}, f32[64,128]{1,0:T(8,128)S(1)}, u32[]{:S(2)}, u32[]{:S(2)}) %collective-permute-start.10) | collective-permute-done | bytes 32800 | tf_op jit(solution)/shard_map/ppermute | solution.py:311
  106.1 2.1 %collective-permute-done.21 = f32[128,128]{1,0:T(8,128)S(1)} collective-permute-done((f32[128,128]{1,0:T(8,128)S(1)}, f32[128,128]{1,0:T(8,128)S(1)}, u32[]{:S(2)}, u32[]{:S(2)}) %collective-permute-start.21) | collective-permute-done | bytes 65568 | tf_op jit(solution)/shard_map/ppermute | solution.py:311
  109.5 8.5 %collective-permute-done.24 = f32[4,128,128]{2,1,0:T(8,128)S(1)} collective-permute-done((f32[4,128,128]{2,1,0:T(8,128)S(1)}, f32[4,128,128]{2,1,0:T(8,128)S(1)}, u32[]{:S(2)}, u32[]{:S(2)}) %collective-permute-start.24) | collective-permute-done | bytes 262176 | tf_op jit(solution)/shard_map/ppermute | solution.py:311
  119.2 3.8 %shard_map.100 = f32[16,2,2,8,8,128]{5,4,3,2,1,0:T(8,128)S(1)} custom-call(s32[1]{0:T(128)} %bitcast.me_ref, f32[16,2,4,8,128]{4,3,2,1,0:T(8,128)S(1)} %bitcast.58, f32[2,4,8,128]{3,2,1,0:T(8,128)S(1)} %bitcast.64, f32[2,4,8,128]{3,2,1,0:T(8,128)S(1)} %bitcast.78, f32[2,4,8,128]{3,2,1,0:T(8,128)S(1)} %bitcast.76, f32[2,4,8,128]{3,2,1,0:T(8,128)S(1)} %bitcast.74, ...), custom_call_target="tpu_custom_call" | custom-call | tf_op jit(solution)/shard_map/pallas_call | solution.py:420
  123.0 36.6 %all_to_all.25.pieces_ref = f32[16,256,128]{2,1,0:T(8,128)S(1)} all-to-all(f32[16,256,128]{2,1,0:T(8,128)S(1)} %bitcast.57), channel_id=1, replica_groups=mesh['band'=16,'grid'=16] {'grid'}, dimensions={0} | all-to-all | bytes 4194304 | tf_op jit(solution)/shard_map/all_to_all | solution.py:307
  159.6 2.4 %shard_map.101 = (f32[2,1,8,128,128]{4,3,2,1,0:T(8,128)}, f32[2,1,8,128,128]{4,3,2,1,0:T(8,128)}) custom-call(f32[16,256,128]{2,1,0:T(8,128)S(1)} %all_to_all.25.pieces_ref, bf16[2,256,256]{2,1,0:T(8,128)(2,1)S(1)} %copy-done.6), custom_call_target="tpu_custom_call" | custom-call | tf_op jit(solution)/shard_map/pallas_call | solution.py:428
  (81 shorter events, 16.5 us)
Async XLA Ops:
  4.8 10.5 %collective-permute-start = (f32[8,64,128]{2,1,0:T(8,128)}, f32[8,64,128]{2,1,0:T(8,128)S(1)}, u32[]{:S(2)}, u32[]{:S(2)}) collective-permute-start(f32[8,64,128]{2,1,0:T(8,128)} %bitcast.96), channel_id=1, source_target_pairs={{0,16},{16,0},{32,48},{48,32},{64,80},{80,64},{96,112},{112,96},{1... | collective-permute-start | bytes 786440 | tf_op jit(solution)/shard_map/ppermute | solution.py:311
  7.0 32.1 %all-to-all-start = ((f32[16,64,128]{2,1,0:T(8,128)}), f32[16,64,128]{2,1,0:T(8,128)S(1)}, u32[]{:S(2)}, u32[]{:S(2)}) async-start(f32[16,64,128]{2,1,0:T(8,128)} %bitcast.87), calls=%async_computation | async-start | bytes 1048576 | tf_op jit(solution)/shard_map/all_to_all | solution.py:307
  16.4 12.3 %collective-permute-start.7 = (f32[64,128]{1,0:T(8,128)S(1)}, f32[64,128]{1,0:T(8,128)S(1)}, u32[]{:S(2)}, u32[]{:S(2)}) collective-permute-start(f32[64,128]{1,0:T(8,128)S(1)} %get-tuple-element.22), channel_id=1, source_target_pairs={{0,224},{16,240},{32,192},{48,208},{64,160},{80,176},{96,128},{112... | collective-permute-start | bytes 98312 | tf_op jit(solution)/shard_map/ppermute | solution.py:311
  19.8 14.2 %collective-permute-start.6 = (f32[64,128]{1,0:T(8,128)S(1)}, f32[64,128]{1,0:T(8,128)S(1)}, u32[]{:S(2)}, u32[]{:S(2)}) collective-permute-start(f32[64,128]{1,0:T(8,128)S(1)} %get-tuple-element.23), channel_id=1, source_target_pairs={{0,192},{16,208},{32,224},{48,240},{64,128},{80,144},{96,160},{112... | collective-permute-start | bytes 98312 | tf_op jit(solution)/shard_map/ppermute | solution.py:311
  21.1 16.9 %collective-permute-start.5 = (f32[64,128]{1,0:T(8,128)S(1)}, f32[64,128]{1,0:T(8,128)S(1)}, u32[]{:S(2)}, u32[]{:S(2)}) collective-permute-start(f32[64,128]{1,0:T(8,128)S(1)} %get-tuple-element.24), channel_id=1, source_target_pairs={{0,160},{16,176},{32,128},{48,144},{64,224},{80,240},{96,192},{112... | collective-permute-start | bytes 98312 | tf_op jit(solution)/shard_map/ppermute | solution.py:311
  24.4 13.6 %collective-permute-start.4 = (f32[64,128]{1,0:T(8,128)S(1)}, f32[64,128]{1,0:T(8,128)S(1)}, u32[]{:S(2)}, u32[]{:S(2)}) collective-permute-start(f32[64,128]{1,0:T(8,128)S(1)} %get-tuple-element.25), channel_id=1, source_target_pairs={{0,128},{16,144},{32,160},{48,176},{64,192},{80,208},{96,224},{112... | collective-permute-start | bytes 98312 | tf_op jit(solution)/shard_map/ppermute | solution.py:311
  25.6 12.4 %collective-permute-start.3 = (f32[64,128]{1,0:T(8,128)S(1)}, f32[64,128]{1,0:T(8,128)S(1)}, u32[]{:S(2)}, u32[]{:S(2)}) collective-permute-start(f32[64,128]{1,0:T(8,128)S(1)} %get-tuple-element.26), channel_id=1, source_target_pairs={{0,96},{16,112},{32,64},{48,80},{64,32},{80,48},{96,0},{112,16},{1... | collective-permute-start | bytes 98312 | tf_op jit(solution)/shard_map/ppermute | solution.py:311
  39.8 16.8 %all-to-all-start.1 = ((f32[16,16,128]{2,1,0:T(8,128)}), f32[16,16,128]{2,1,0:T(8,128)S(1)}, u32[]{:S(2)}, u32[]{:S(2)}) async-start(f32[16,16,128]{2,1,0:T(8,128)} %get-tuple-element.15), calls=%async_computation.1 | async-start | bytes 262144 | tf_op jit(solution)/shard_map/all_to_all | solution.py:307
  49.6 55.9 %collective-permute-start.22 = (f32[128,128]{1,0:T(8,128)S(1)}, f32[128,128]{1,0:T(8,128)S(1)}, u32[]{:S(2)}, u32[]{:S(2)}) collective-permute-start(f32[128,128]{1,0:T(8,128)S(1)} %get-tuple-element.18), channel_id=1, source_target_pairs={{0,224},{16,240},{32,192},{48,208},{64,160},{80,176},{96,128},{112... | collective-permute-start | bytes 196616 | tf_op jit(solution)/shard_map/ppermute | solution.py:311
  50.2 15.6 %collective-permute-start.19 = (f32[128,128]{1,0:T(8,128)S(1)}, f32[128,128]{1,0:T(8,128)S(1)}, u32[]{:S(2)}, u32[]{:S(2)}) collective-permute-start(f32[128,128]{1,0:T(8,128)S(1)} %get-tuple-element.18), channel_id=1, source_target_pairs={{0,128},{16,144},{32,160},{48,176},{64,192},{80,208},{96,224},{112... | collective-permute-start | bytes 196616 | tf_op jit(solution)/shard_map/ppermute | solution.py:311
  54.0 11.8 %collective-permute-start.18 = (f32[128,128]{1,0:T(8,128)S(1)}, f32[128,128]{1,0:T(8,128)S(1)}, u32[]{:S(2)}, u32[]{:S(2)}) collective-permute-start(f32[128,128]{1,0:T(8,128)S(1)} %get-tuple-element.18), channel_id=1, source_target_pairs={{0,64},{16,80},{32,96},{48,112},{64,0},{80,16},{96,32},{112,48},{1... | collective-permute-start | bytes 196616 | tf_op jit(solution)/shard_map/ppermute | solution.py:311
  57.7 15.4 %all-to-all-start.2 = ((f32[16,8,128]{2,1,0:T(8,128)}), f32[16,8,128]{2,1,0:T(8,128)S(1)}, u32[]{:S(2)}, u32[]{:S(2)}) async-start(f32[16,8,128]{2,1,0:T(8,128)} %shard_map.97), calls=%async_computation.2 | async-start | bytes 131072 | tf_op jit(solution)/shard_map/all_to_all | solution.py:307
  74.0 12.8 %collective-permute-start.14 = (f32[64,128]{1,0:T(8,128)S(1)}, f32[64,128]{1,0:T(8,128)S(1)}, u32[]{:S(2)}, u32[]{:S(2)}) collective-permute-start(f32[64,128]{1,0:T(8,128)S(1)} %get-tuple-element.17), channel_id=1, source_target_pairs={{0,224},{16,240},{32,192},{48,208},{64,160},{80,176},{96,128},{112... | collective-permute-start | bytes 98312 | tf_op jit(solution)/shard_map/ppermute | solution.py:311
  74.7 13.8 %collective-permute-start.13 = (f32[64,128]{1,0:T(8,128)S(1)}, f32[64,128]{1,0:T(8,128)S(1)}, u32[]{:S(2)}, u32[]{:S(2)}) collective-permute-start(f32[64,128]{1,0:T(8,128)S(1)} %get-tuple-element.17), channel_id=1, source_target_pairs={{0,192},{16,208},{32,224},{48,240},{64,128},{80,144},{96,160},{112... | collective-permute-start | bytes 98312 | tf_op jit(solution)/shard_map/ppermute | solution.py:311
  79.0 11.5 %collective-permute-start.12 = (f32[64,128]{1,0:T(8,128)S(1)}, f32[64,128]{1,0:T(8,128)S(1)}, u32[]{:S(2)}, u32[]{:S(2)}) collective-permute-start(f32[64,128]{1,0:T(8,128)S(1)} %get-tuple-element.17), channel_id=1, source_target_pairs={{0,160},{16,176},{32,128},{48,144},{64,224},{80,240},{96,192},{112... | collective-permute-start | bytes 98312 | tf_op jit(solution)/shard_map/ppermute | solution.py:311
  79.2 11.5 %collective-permute-start.11 = (f32[64,128]{1,0:T(8,128)S(1)}, f32[64,128]{1,0:T(8,128)S(1)}, u32[]{:S(2)}, u32[]{:S(2)}) collective-permute-start(f32[64,128]{1,0:T(8,128)S(1)} %get-tuple-element.17), channel_id=1, source_target_pairs={{0,128},{16,144},{32,160},{48,176},{64,192},{80,208},{96,224},{112... | collective-permute-start | bytes 98312 | tf_op jit(solution)/shard_map/ppermute | solution.py:311
  82.1 37.1 %all-to-all-start.3 = ((f32[16,64,128]{2,1,0:T(8,128)}), f32[16,64,128]{2,1,0:T(8,128)S(1)}, u32[]{:S(2)}, u32[]{:S(2)}) async-start(f32[16,64,128]{2,1,0:T(8,128)} %get-tuple-element.16), calls=%async_computation.3 | async-start | bytes 1048576 | tf_op jit(solution)/shard_map/all_to_all | solution.py:307
  86.8 21.3 %collective-permute-start.20 = (f32[2,128,128]{2,1,0:T(8,128)S(1)}, f32[2,128,128]{2,1,0:T(8,128)S(1)}, u32[]{:S(2)}, u32[]{:S(2)}) collective-permute-start(f32[2,128,128]{2,1,0:T(8,128)S(1)} %pad_maximum_fusion.5), channel_id=1, source_target_pairs={{0,32},{16,48},{32,0},{48,16},{64,96},{80,112},{96,64},{112,80},{1... | collective-permute-start | bytes 393224 | tf_op jit(solution)/shard_map/ppermute | solution.py:311
  88.5 15.0 %collective-permute-start.10 = (f32[64,128]{1,0:T(8,128)S(1)}, f32[64,128]{1,0:T(8,128)S(1)}, u32[]{:S(2)}, u32[]{:S(2)}) collective-permute-start(f32[64,128]{1,0:T(8,128)S(1)} %get-tuple-element.17), channel_id=1, source_target_pairs={{0,96},{16,112},{32,64},{48,80},{64,32},{80,48},{96,0},{112,16},{1... | collective-permute-start | bytes 98312 | tf_op jit(solution)/shard_map/ppermute | solution.py:311
  90.6 12.9 %collective-permute-start.9 = (f32[64,128]{1,0:T(8,128)S(1)}, f32[64,128]{1,0:T(8,128)S(1)}, u32[]{:S(2)}, u32[]{:S(2)}) collective-permute-start(f32[64,128]{1,0:T(8,128)S(1)} %get-tuple-element.17), channel_id=1, source_target_pairs={{0,64},{16,80},{32,96},{48,112},{64,0},{80,16},{96,32},{112,48},{1... | collective-permute-start | bytes 98312 | tf_op jit(solution)/shard_map/ppermute | solution.py:311
  90.7 13.8 %collective-permute-start.8 = (f32[64,128]{1,0:T(8,128)S(1)}, f32[64,128]{1,0:T(8,128)S(1)}, u32[]{:S(2)}, u32[]{:S(2)}) collective-permute-start(f32[64,128]{1,0:T(8,128)S(1)} %get-tuple-element.17), channel_id=1, source_target_pairs={{0,32},{16,48},{32,0},{48,16},{64,96},{80,112},{96,64},{112,80},{1... | collective-permute-start | bytes 98312 | tf_op jit(solution)/shard_map/ppermute | solution.py:311
  104.5 14.6 %collective-permute-start.16 = (f32[4,64,128]{2,1,0:T(8,128)S(1)}, f32[4,64,128]{2,1,0:T(8,128)S(1)}, u32[]{:S(2)}, u32[]{:S(2)}) collective-permute-start(f32[4,64,128]{2,1,0:T(8,128)S(1)} %pad_maximum_fusion.4), channel_id=1, source_target_pairs={{0,16},{16,0},{32,48},{48,32},{64,80},{80,64},{96,112},{112,96},{1... | collective-permute-start | bytes 393224 | tf_op jit(solution)/shard_map/ppermute | solution.py:311
  105.5 13.6 %collective-permute-start.15 = (f32[4,64,128]{2,1,0:T(8,128)S(1)}, f32[4,64,128]{2,1,0:T(8,128)S(1)}, u32[]{:S(2)}, u32[]{:S(2)}) collective-permute-start(f32[4,64,128]{2,1,0:T(8,128)S(1)} %pad_maximum_fusion.3), channel_id=1, source_target_pairs={{0,16},{16,0},{32,48},{48,32},{64,80},{80,64},{96,112},{112,96},{1... | collective-permute-start | bytes 393224 | tf_op jit(solution)/shard_map/ppermute | solution.py:311
  108.2 9.7 %collective-permute-start.24 = (f32[4,128,128]{2,1,0:T(8,128)S(1)}, f32[4,128,128]{2,1,0:T(8,128)S(1)}, u32[]{:S(2)}, u32[]{:S(2)}) collective-permute-start(f32[4,128,128]{2,1,0:T(8,128)S(1)} %pad_maximum_fusion.2), channel_id=1, source_target_pairs={{0,16},{16,0},{32,48},{48,32},{64,80},{80,64},{96,112},{112,96},{1... | collective-permute-start | bytes 786440 | tf_op jit(solution)/shard_map/ppermute | solution.py:311
  (12 other events, 291.7 us)
